TPU v7x, 64 devices: a 2x2x8 block of a 4x4x8 slice. The times are simulated.
64 devices in a mesh: rep: 4 (over x, y), data: 16 (over z, core).
Axes of the slice: x: 2, y: 2, z: 8, core: 2. Of those that a mesh axis runs over, the one named last changes fastest.
The devices are a block of a 4x4x8 slice.
Arguments:
- x: bfloat16 [8192, 4096], P(('rep', 'data')), parts along dimension 0
- adapter_id: int32 [8192], P(('rep', 'data')), parts along dimension 0
- dout: bfloat16 [8192, 4096], P(('rep', 'data')), parts along dimension 0
- w_gate: bfloat16 [4096, 14336], replicated
- w_up: bfloat16 [4096, 14336], replicated
- w_down: bfloat16 [14336, 4096], replicated
- a_gate: bfloat16 [32, 4096, 16], P('data')
- b_gate: bfloat16 [32, 16, 14336], P('data')
- a_up: bfloat16 [32, 4096, 16], P('data')
- b_up: bfloat16 [32, 16, 14336], P('data')
- a_down: bfloat16 [32, 14336, 16], P('data')
- b_down: bfloat16 [32, 16, 4096], P('data')
Outputs:
- output 1: bfloat16 [8192, 4096], P(('rep', 'data')), parts along dimension 0
- output 2: bfloat16 [8192, 4096], P(('rep', 'data')), parts along dimension 0
- output 3: float32 [128, 4096, 16], P(('rep', 'data')), parts along dimension 0
- output 4: float32 [128, 16, 14336], P(('rep', 'data')), parts along dimension 0
- output 5: float32 [128, 4096, 16], P(('rep', 'data')), parts along dimension 0
- output 6: float32 [128, 16, 14336], P(('rep', 'data')), parts along dimension 0
- output 7: float32 [128, 14336, 16], P(('rep', 'data')), parts along dimension 0
- output 8: float32 [128, 16, 4096], P(('rep', 'data')), parts along dimension 0
There are 4 independent parts. A program takes and returns all parts, laid end to end along the dimension named above; an argument that names none is the same for every part.
All inputs are finite; a program needn't handle non-finite values.
Results may differ from a plain program's by a relative error of at most 0.00124.
Values are sent between devices in bfloat16 or wider.
A program may use at most 768 MiB of HBM per device.

v0:
```python
import functools

import jax
import jax.numpy as jnp
from jax import lax
from jax.experimental import pallas as pl
from jax.experimental.pallas import tpu as pltpu
from jax.sharding import PartitionSpec as P


LORA_ALPHA = 32
LANES = 128
CHUNK = 1024
LO = 256
F32 = jnp.float32
BF16 = jnp.bfloat16
Shape = jax.ShapeDtypeStruct
HBM = pl.BlockSpec(memory_space=pl.ANY)


def nn(a, b):
    return lax.dot_general(a, b, (((1,), (0,)), ((), ())), preferred_element_type=F32)


def nt(a, b):
    return lax.dot_general(a, b, (((1,), (1,)), ((), ())), preferred_element_type=F32)


def tn(a, b):
    return lax.dot_general(a, b, (((0,), (0,)), ((), ())), preferred_element_type=F32)


def rounded(v):
    return v.astype(BF16).astype(F32)


def both(a, b, c=slice(None)):
    return jnp.concatenate([a[:, c], b[:, c]], axis=0)


def update_both(a, b, v, block, c=slice(None)):
    half = a.shape[0]
    update(a, c, v[:half], block)
    update(b, c, v[half:], block)


def pieces(width, size):
    return [slice(j, j + size) for j in range(0, width, size)]


def row_blocks(n, rows, body, when=None):
    ok = n >= 0 if when is None else when
    pl.when(ok)(functools.partial(body, slice(0, LO), 0))
    pl.when(ok & (n > LO))(functools.partial(body, slice(LO, rows), 1))


def update(ref, c, v, block):
    ref[:, c] = v if block == 0 else ref[:, c] + v


def at_col(ref, tile):
    return lambda t: ref.at[:, pl.ds(pl.multiple_of(t * tile, tile), tile)]


def at_row(ref, tile):
    return lambda t: ref.at[pl.ds(pl.multiple_of(t * tile, tile), tile), :]


def ring(i, steps, items, sems):
    depth = items[0][1].shape[0]

    def copy(t, s, which):
        src, buf = items[which]
        return pltpu.make_async_copy(src(t), buf.at[s], sems.at[which, s])

    @pl.when(i == 0)
    def _():
        for t in range(depth - 1):
            for which in range(len(items)):
                copy(t, t, which).start()

    ahead = i + depth - 1

    @pl.when(ahead < steps)
    def _():
        for which in range(len(items)):
            copy(ahead, lax.rem(ahead, depth), which).start()

    slot = lax.rem(i, depth)
    for which in range(len(items)):
        copy(i, slot, which).wait()
    return [buf.at[slot] for _, buf in items]


def whole(shape):
    return pl.BlockSpec(shape, lambda i, n: (0, 0), pipeline_mode=pl.Buffered(1))


def col(rows, tile):
    return pl.BlockSpec((rows, tile), lambda i, n: (0, i))


def rows_pair(rows, tile):
    upper = pl.BlockSpec((rows - LO, tile), lambda i, n: (0, jnp.where(n[0] > LO, i, 0)))
    return [col(LO, tile), upper]


def pair_shape(rows, width, dtype):
    return [Shape((LO, width), dtype), Shape((rows - LO, width), dtype)]


def call(body, n, steps, args, in_specs, out_shape, out_specs, scratch, products, weight_bytes):
    return pl.pallas_call(
        body,
        grid_spec=pltpu.PrefetchScalarGridSpec(
            num_scalar_prefetch=1, grid=(steps,), in_specs=in_specs, out_specs=out_specs, scratch_shapes=scratch
        ),
        out_shape=out_shape,
        compiler_params=pltpu.CompilerParams(dimension_semantics=('arbitrary',), vmem_limit_bytes=63_000_000),
        cost_estimate=pl.CostEstimate(flops=LO * weight_bytes * products, bytes_accessed=weight_bytes, transcendentals=0),
    )(n, *args)


def fwd_kernel(
    scale, n_ref, xr_ref, pack_ref, spread_ref, ag0, ag1, au0, au1, bd0, bd1, wg_hbm, wu_hbm, wd_hbm, bg0, bg1, bu0, bu1, ad0, ad1,
    out_ref, xs, mask_ref, pgt_ref, put_ref, pdt_ref, g_lo, g_hi, u_lo, u_hi,
    xbuf, oacc, pg_s, pu_s, pd_s, wgb, wub, wdb, wsem, sem,
):
    i = pl.program_id(0)
    last = pl.num_programs(0) - 1
    n = n_ref[0]
    rows, width = xs.shape
    k = pg_s.shape[1]

    @pl.when(i == 0)
    def _():
        pltpu.make_async_copy(xr_ref, xbuf, sem).start()

    tile = wgb.shape[2]
    weights = [(at_col(wg_hbm, tile), wgb), (at_col(wu_hbm, tile), wub), (at_row(wd_hbm, tile), wdb)]
    wg, wu, wd = ring(i, last + 1, weights, wsem)

    @pl.when(i == 0)
    def _():
        pltpu.make_async_copy(xr_ref, xbuf, sem).wait()

    def start(r, block):
        take = pack_ref[r, :]
        for e in pieces(width, CHUNK):
            xs[r, e] = nn(take, xbuf[:, e]).astype(BF16)
        mask_ref[r, :] = nn(take, xbuf[:, width:])[:, :k]
        keep = mask_ref[r, :] > 0
        x = xs[r, :]
        for a, b, s, t in ((ag0, ag1, pg_s, pgt_ref), (au0, au1, pu_s, put_ref)):
            p = jnp.where(keep, nt(x, both(a, b)), 0.0)
            s[r, :] = p.astype(BF16)
            t[:, r] = p.T.astype(BF16)
        oacc[r, :] = jnp.zeros(x.shape, F32)
        pd_s[r, :] = jnp.zeros(keep.shape, F32)

    def step(r, block):
        x = xs[r, :]
        g = nn(x, wg[...]) + rounded(scale * nn(pg_s[r, :], both(bg0, bg1)))
        u = nn(x, wu[...]) + rounded(scale * nn(pu_s[r, :], both(bu0, bu1)))
        (g_lo, g_hi)[block][...] = g
        (u_lo, u_hi)[block][...] = u
        h = (g * jax.nn.sigmoid(g) * u).astype(BF16)
        for e in pieces(width, CHUNK):
            oacc[r, e] += nn(h, wd[:, e])
        pd_s[r, :] += nt(h, both(ad0, ad1))

    def finish(r, block):
        pd = jnp.where(mask_ref[r, :] > 0, pd_s[r, :], 0.0)
        pdt_ref[:, r] = pd.T.astype(BF16)
        pdb = pd.astype(BF16)
        spread = spread_ref[:, r]
        for e in pieces(width, CHUNK):
            out = xs[r, e].astype(F32) + oacc[r, e] + rounded(scale * nn(pdb, both(bd0, bd1, e)))
            update(xbuf, e, nn(spread, out.astype(BF16)).astype(BF16), block)

    row_blocks(n, rows, start, i == 0)
    row_blocks(n, rows, step)
    row_blocks(n, rows, finish, i == last)

    @pl.when(i == last)
    def _():
        save = pltpu.make_async_copy(xbuf.at[:, pl.ds(0, width)], out_ref, sem)
        save.start()
        save.wait()


def fwd(scale, n, xr, pack, spread, ag, au, bd, wg, wu, wd, bg, bu, ad, tile=512, depth=3):
    rows = xr.shape[0]
    width, hidden = wg.shape
    half = ag[0].shape[0]
    k = 2 * half
    return call(
        functools.partial(fwd_kernel, scale), n, hidden // tile,
        (xr, pack, spread, *ag, *au, *bd, wg, wu, wd, *bg, *bu, *ad),
        [HBM] + [whole((rows, rows))] * 2 + [whole((half, width))] * 6 + [HBM] * 3 + [col(half, tile)] * 6,
        [Shape((rows, width), BF16)] * 2 + [Shape((rows, k), F32)] + [Shape((k, rows), BF16)] * 3 + pair_shape(rows, hidden, F32) * 2,
        [HBM, whole((rows, width)), whole((rows, k))] + [whole((k, rows))] * 3 + rows_pair(rows, tile) * 2,
        [pltpu.VMEM(xr.shape, BF16), pltpu.VMEM((rows, width), F32)] + [pltpu.VMEM((rows, k), BF16)] * 2 + [pltpu.VMEM((rows, k), F32)]
        + [pltpu.VMEM((depth, width, tile), BF16)] * 2 + [pltpu.VMEM((depth, tile, width), BF16)]
        + [pltpu.SemaphoreType.DMA((3, depth)), pltpu.SemaphoreType.DMA],
        1, 6 * width * hidden,
    )


def bwd_kernel(
    scale, n_ref, dr_ref, pack_ref, xs_ref, mask_ref, pgt_ref, put_ref, pdt_ref, bd0, bd1,
    wd_hbm, g_lo, g_hi, u_lo, u_hi, bg0, bg1, bu0, bu1, ad0, ad1,
    ds, qg_ref, qu_ref, gag0, gag1, gau0, gau1, gbd0, gbd1, dg_lo, dg_hi, du_lo, du_hi, gbg0, gbg1, gbu0, gbu1, gad0, gad1,
    dbuf, qd_s, qdt_s, qg_s, qu_s, wdb, wsem, sem,
):
    i = pl.program_id(0)
    last = pl.num_programs(0) - 1
    n = n_ref[0]
    rows, width = ds.shape

    @pl.when(i == 0)
    def _():
        pltpu.make_async_copy(dr_ref, dbuf, sem).start()

    wd, = ring(i, last + 1, [(at_row(wd_hbm, wdb.shape[1]), wdb)], wsem)

    @pl.when(i == 0)
    def _():
        pltpu.make_async_copy(dr_ref, dbuf, sem).wait()

    def start(r, block):
        take = pack_ref[r, :]
        for e in pieces(width, CHUNK):
            ds[r, e] = nn(take, dbuf[:, e]).astype(BF16)
        qd = jnp.where(mask_ref[r, :] > 0, scale * nt(ds[r, :], both(bd0, bd1)), 0.0)
        qd_s[r, :] = qd.astype(BF16)
        qdt_s[:, r] = qd.T.astype(BF16)
        for s in (qg_s, qu_s):
            s[r, :] = jnp.zeros(qd.shape, F32)

    def step(r, block):
        for c in pieces(wd.shape[0], CHUNK // 2):
            bg, bu, ad = both(bg0, bg1, c), both(bu0, bu1, c), both(ad0, ad1, c)
            dh = nt(ds[r, :], wd[c, :]) + rounded(nn(qd_s[r, :], ad))
            g = (g_lo, g_hi)[block][:, c]
            u = (u_lo, u_hi)[block][:, c]
            sig = jax.nn.sigmoid(g)
            act = g * sig
            h = (act * u).astype(BF16)
            dg = (dh * u * sig * (1.0 + g * (1.0 - sig))).astype(BF16)
            du = (dh * act).astype(BF16)
            (dg_lo, dg_hi)[block][:, c] = dg
            (du_lo, du_hi)[block][:, c] = du
            qg_s[r, :] += nt(dg, bg)
            qu_s[r, :] += nt(du, bu)
            update_both(gbg0, gbg1, scale * nn(pgt_ref[:, r], dg), block, c)
            update_both(gbu0, gbu1, scale * nn(put_ref[:, r], du), block, c)
            update_both(gad0, gad1, nn(qdt_s[:, r], h), block, c)

    def finish(r, block):
        keep = mask_ref[r, :] > 0
        qg = jnp.where(keep, scale * qg_s[r, :], 0.0)
        qu = jnp.where(keep, scale * qu_s[r, :], 0.0)
        qg_ref[r, :] = qg.astype(BF16)
        qu_ref[r, :] = qu.astype(BF16)
        qgt, qut, pdt = qg.T.astype(BF16), qu.T.astype(BF16), pdt_ref[:, r]
        for e in pieces(width, CHUNK):
            update_both(gag0, gag1, nn(qgt, xs_ref[r, e]), block, e)
            update_both(gau0, gau1, nn(qut, xs_ref[r, e]), block, e)
            update_both(gbd0, gbd1, scale * nn(pdt, ds[r, e]), block, e)

    row_blocks(n, rows, start, i == 0)
    row_blocks(n, rows, step)
    row_blocks(n, rows, finish, i == last)

    @pl.when(n <= LO)
    def _():
        for ref in (dg_hi, du_hi):
            ref[...] = jnp.zeros(ref.shape, BF16)

    @pl.when((n <= LO) & (i == last))
    def _():
        for ref in (ds, qg_ref, qu_ref):
            ref[LO:, :] = jnp.zeros((rows - LO, ref.shape[1]), BF16)


def bwd(scale, n, dr, pack, xs, mask, pgt, put, pdt, bd, wd, g, u, bg, bu, ad, tile=1024, depth=3):
    rows, width = dr.shape
    hidden = wd.shape[0]
    half = bd[0].shape[0]
    k = 2 * half
    pair = rows_pair(rows, tile)
    return call(
        functools.partial(bwd_kernel, scale), n, hidden // tile,
        (dr, pack, xs, mask, pgt, put, pdt, *bd, wd, *g, *u, *bg, *bu, *ad),
        [HBM, whole((rows, rows)), whole((rows, width)), whole((rows, k))] + [whole((k, rows))] * 3 + [whole((half, width))] * 2
        + [HBM] + pair * 2 + [col(half, tile)] * 6,
        [Shape((rows, width), BF16)] + [Shape((rows, k), BF16)] * 2 + [Shape((half, width), F32)] * 6
        + pair_shape(rows, hidden, BF16) * 2 + [Shape((half, hidden), F32)] * 6,
        [whole((rows, width))] + [whole((rows, k))] * 2 + [whole((half, width))] * 6 + [col(LO, tile), col(rows - LO, tile)] * 2
        + [col(half, tile)] * 6,
        [pltpu.VMEM((rows, width), BF16), pltpu.VMEM((rows, k), BF16), pltpu.VMEM((k, rows), BF16)]
        + [pltpu.VMEM((rows, k), F32)] * 2 + [pltpu.VMEM((depth, tile, width), BF16)]
        + [pltpu.SemaphoreType.DMA((1, depth)), pltpu.SemaphoreType.DMA],
        1, 2 * width * hidden,
    )


def dx_kernel(
    parts, ds_ref, spread_ref, qg_ref, qu_ref, ag0, ag1, au0, au1, wg_hbm, wu_hbm, dg_lo, dg_hi, du_lo, du_hi,
    back_ref, acc, dgs, dus, sendbuf, wgb, wub, wsem, psem, send_sem, recv_sem, own_sem,
):
    i = pl.program_id(0)
    total = pl.num_programs(0)
    steps = total // parts
    q, t = i // steps, lax.rem(i, steps)
    _, width = ds_ref.shape
    tile = wgb.shape[2]
    part = width // parts
    group, cap = back_ref.shape[:2]
    me = lax.axis_index('data')
    peers = [lax.rem(me + k, group) for k in range(1, group)]
    barrier = pltpu.get_barrier_semaphore()

    @pl.when(i == 0)
    def _():
        for peer in peers:
            pl.semaphore_signal(barrier, inc=1, device_id={'data': peer}, device_id_type=pl.DeviceIdType.MESH)

    def weight(ref):
        def src(s):
            r = pl.multiple_of(s // steps * part, part)
            c = pl.multiple_of(lax.rem(s, steps) * tile, tile)
            return ref.at[pl.ds(r, part), pl.ds(c, tile)]

        return src

    wg, wu = ring(i, total, [(weight(wg_hbm), wgb), (weight(wu_hbm), wub)], wsem)

    def cols(s):
        return pl.ds(pl.multiple_of(s * tile, tile), tile)

    def fills(s):
        pairs = ((dg_lo, dgs, 0), (dg_hi, dgs, LO), (du_lo, dus, 0), (du_hi, dus, LO))
        return [
            pltpu.make_async_copy(src.at[:, cols(s)], dst.at[pl.ds(r, src.shape[0]), cols(s)], psem.at[j, s])
            for j, (src, dst, r) in enumerate(pairs)
        ]

    @pl.when(i == 0)
    def _():
        for s in range(2):
            for copy in fills(s):
                copy.start()

    @pl.when(i + 2 < steps)
    def _():
        for copy in fills(i + 2):
            copy.start()

    @pl.when(i < steps)
    def _():
        for copy in fills(i):
            copy.wait()

    @pl.when(t == 0)
    def _():
        acc[...] = jnp.zeros(acc.shape, F32)

    dg = dgs[:, cols(t)]
    du = dus[:, cols(t)]
    for e in pieces(part, CHUNK // 2):
        acc[:, e] += nt(dg, wg[e, :]) + nt(du, wu[e, :])

    def here(s):
        return pl.ds(pl.multiple_of(s * part, part), part)

    def sends(s):
        return [
            pltpu.make_async_remote_copy(
                src_ref=sendbuf.at[s, peer], dst_ref=back_ref.at[me, :, here(s)], send_sem=send_sem.at[s, peer],
                recv_sem=recv_sem.at[s, me], device_id={'data': peer}, device_id_type=pl.DeviceIdType.MESH,
            )
            for peer in peers
        ]

    def arrivals(s):
        return [
            pltpu.make_async_remote_copy(
                src_ref=sendbuf.at[s, peer], dst_ref=back_ref.at[peer, :, here(s)], send_sem=send_sem.at[s, peer],
                recv_sem=recv_sem.at[s, peer], device_id={'data': peer}, device_id_type=pl.DeviceIdType.MESH,
            )
            for peer in peers
        ]

    def keep(s):
        return pltpu.make_async_copy(sendbuf.at[s, me], back_ref.at[me, :, here(s)], own_sem.at[s])

    @pl.when(t == steps - 1)
    def _():
        c = here(q)
        lora = rounded(nn(qg_ref[...], both(ag0, ag1, c)) + nn(qu_ref[...], both(au0, au1, c)))
        dx = (ds_ref[:, c].astype(F32) + acc[...] + lora).astype(BF16)
        spread = nn(spread_ref[...], dx)
        for p in range(group):
            sendbuf[q, p] = spread[p * cap : (p + 1) * cap].astype(BF16)

        @pl.when(q == 0)
        def _():
            pl.semaphore_wait(barrier, group - 1)

        for copy in sends(q):
            copy.start()
        keep(q).start()

    @pl.when(i == total - 1)
    def _():
        for s in range(parts):
            keep(s).wait()
            for copy in sends(s):
                copy.wait_send()
            for copy in arrivals(s):
                copy.wait_recv()


def dx_all(group, ds, spread, qg, qu, ag, au, wg, wu, dg, du, parts=4, tile=2048, depth=3):
    rows, width = ds.shape
    hidden = wg.shape[1]
    half, k = ag[0].shape[0], qg.shape[1]
    part, cap = width // parts, rows // group
    steps = hidden // tile

    def fixed(shape):
        return pl.BlockSpec(shape, lambda i: (0, 0), pipeline_mode=pl.Buffered(1))

    dma = pltpu.SemaphoreType.DMA
    back = pl.pallas_call(
        functools.partial(dx_kernel, parts),
        grid=(parts * steps,),
        in_specs=[fixed((rows, width)), fixed((rows, rows))] + [fixed((rows, k))] * 2 + [fixed((half, width))] * 4 + [HBM] * 6,
        out_specs=HBM,
        out_shape=Shape((group, cap, width), BF16),
        scratch_shapes=[pltpu.VMEM((rows, part), F32)] + [pltpu.VMEM((rows, hidden), BF16)] * 2 + [pltpu.VMEM((parts, group, cap, part), BF16)]
        + [pltpu.VMEM((depth, part, tile), BF16)] * 2
        + [dma((2, depth)), dma((4, steps)), dma((parts, group)), dma((parts, group)), dma((parts,))],
        compiler_params=pltpu.CompilerParams(
            dimension_semantics=('arbitrary',), vmem_limit_bytes=63_000_000, collective_id=0, has_side_effects=True
        ),
        cost_estimate=pl.CostEstimate(flops=4 * rows * width * hidden, bytes_accessed=4 * width * hidden, transcendentals=0),
    )(ds, spread, qg, qu, *ag, *au, wg, wu, *dg, *du)
    return back.reshape(rows, width)


def solution(mesh):
    group = mesh.shape['data']
    tok = P(('rep', 'data'), None)
    ids_spec = P(('rep', 'data'))
    full = P(None, None)
    own = P('data', None, None)
    grad = P(('rep', 'data'), None, None)
    swap = [(i, i ^ 1) for i in range(group)]

    def layer(x, ids, dy, w_gate, w_up, w_down, a_gate, b_gate, a_up, b_up, a_down, b_down):
        tokens, width = x.shape
        n_local, _, rank = a_gate.shape
        scale = LORA_ALPHA / rank
        cap = ((3 * tokens + 8 * group - 1) // (8 * group)) * 8
        slots = group * cap
        part = cap // 2
        half = n_local * rank
        iota = functools.partial(lax.broadcasted_iota, jnp.int32)

        owner = ids // n_local
        earlier = iota((tokens, tokens), 0) > iota((tokens, tokens), 1)
        order = jnp.sum(jnp.where(earlier & (owner[:, None] == owner[None, :]), 1, 0), axis=1)
        core = (order + owner // 2 + lax.axis_index('data')) % 2
        dest = ((owner // 2) * 2 + core) * cap + (owner % 2) * part + order // 2
        send = (iota((slots, tokens), 0) == dest[None, :]).astype(BF16)
        column = iota((tokens, LANES), 1)
        first = ((owner % 2) ^ core) * half + (ids % n_local) * rank
        flags = ((column >= first[:, None]) & (column < first[:, None] + rank)).astype(BF16)

        def exchange(rows):
            return lax.all_to_all(rows, 'data', 0, 0, tiled=True)

        xr = exchange(nn(send, jnp.concatenate([x, flags], axis=1)).astype(BF16))
        packed_dy, xr = lax.optimization_barrier((nn(send, dy).astype(BF16), xr))
        dr = exchange(packed_dy)

        valid = jnp.sum(xr[:, width:].astype(F32), axis=1) > 0
        upto = (iota((slots, slots), 0) >= iota((slots, slots), 1)) & valid[None, :]
        place = jnp.where(valid, jnp.sum(jnp.where(upto, 1, 0), axis=1) - 1, -1)
        count = jnp.sum(jnp.where(valid, 1, 0)).astype(jnp.int32).reshape(1)
        pack = (place[None, :] == iota((slots, slots), 0)).astype(BF16)
        spread = (place[:, None] == iota((slots, slots), 1)).astype(BF16)

        def flat_a(a):
            v = jnp.swapaxes(a, 1, 2).reshape(half, a.shape[1])
            return v, lax.ppermute(v, 'data', swap)

        def flat_b(b):
            v = b.reshape(half, b.shape[2])
            return v, lax.ppermute(v, 'data', swap)

        ag, au, ad = flat_a(a_gate), flat_a(a_up), flat_a(a_down)
        bg, bu, bd = flat_b(b_gate), flat_b(b_up), flat_b(b_down)

        out_rows, xs, mask, pgt, put, pdt, *gu = fwd(scale, count, xr, pack, spread, ag, au, bd, w_gate, w_up, w_down, bg, bu, ad)
        res = bwd(scale, count, dr, pack, xs, mask, pgt, put, pdt, bd, w_down, gu[:2], gu[2:], bg, bu, ad)
        ds, qg, qu = res[:3]
        dg, du = res[9:11], res[11:13]
        back = [exchange(out_rows)]
        back.append(dx_all(group, ds, spread, qg, qu, ag, au, w_gate, w_up, dg, du))
        sums = [res[j] + lax.ppermute(res[j + 1], 'data', swap) for j in (3, 5, 7, 13, 15, 17)]
        gag, gau, gbd, gbg, gbu, gad = sums

        def shape_a(v):
            return jnp.swapaxes(v.reshape(n_local, rank, v.shape[1]), 1, 2)

        def shape_b(v):
            return v.reshape(n_local, rank, v.shape[1])

        out, dx = [tn(send, v).astype(BF16) for v in back]
        return out, dx, shape_a(gag), shape_b(gbg), shape_a(gau), shape_b(gbu), shape_a(gad), shape_b(gbd)

    return jax.shard_map(
        layer,
        mesh=mesh,
        in_specs=(tok, ids_spec, tok, full, full, full, own, own, own, own, own, own),
        out_specs=(tok, tok, grad, grad, grad, grad, grad, grad),
        check_vma=False,
    )
```

profile of v0, /device:TPU:53, one launch (start us, length us, event | category | flops | bytes accessed | tf_op | source)
XLA Modules:
  0.0 467.8 jit_solution(16927010580358004652)
XLA Ops:
  0.7 0.8 and_select_fusion.5
  1.4 0.2 select_reduce_fusion.1
  1.6 0.7 broadcast_add_fusion
  2.3 0.7 fusion.16
  3.1 3.9 convolution_convert_fusion
  7.0 9.5 %all-to-all-start = ((bf16[16,24,4224]{2,1,0:T(8,128)(2,1)}), bf16[16,24,4224]{2,1,0:T(8,128)(2,1)}, u32[]{:S(2)}, u32[]{:S(2)}) async-start(bf16[16,24,4224]{2,1,0:T(8,128)(2,1)} %bitcast.35), calls=%async_computation | async-start | bytes 6488064 | tf_op jit(solution)/shard_map/all_to_all | solution.py:484
  16.5 0.5 collective-permute-start
  17.2 0.4 collective-permute-start.3
  17.7 0.4 collective-permute-start.5
  18.1 2.7 convolution_convert_fusion.1
  20.8 67.9 %all-to-all-done = bf16[16,24,4224]{2,1,0:T(8,128)(2,1)} async-done(((bf16[16,24,4224]{2,1,0:T(8,128)(2,1)}), bf16[16,24,4224]{2,1,0:T(8,128)(2,1)}, u32[]{:S(2)}, u32[]{:S(2)}) %all-to-all-start) | async-done | bytes 3244064 | tf_op jit(solution)/shard_map/all_to_all | solution.py:484
  88.7 1.0 convert_reduce_fusion
  89.7 0.7 select_reduce_fusion.2
  90.5 0.2 collective-permute-start.2
  90.8 6.5 %all-to-all-start.2 = ((bf16[16,24,4096]{2,1,0:T(8,128)(2,1)}), bf16[16,24,4096]{2,1,0:T(8,128)(2,1)}, u32[]{:S(2)}, u32[]{:S(2)}) async-start(bf16[16,24,4096]{2,1,0:T(8,128)(2,1)} %bitcast.36), calls=%async_computation.2 | async-start | bytes 6291456 | tf_op jit(solution)/shard_map/all_to_all | solution.py:484
  97.2 0.9 fusion.5
  98.2 0.7 copy-done.9
  98.9 134.9 %shard_map.179 = (bf16[384,4096]{1,0:T(8,128)(2,1)}, bf16[384,4096]{1,0:T(8,128)(2,1)}, f32[384,64]{1,0:T(8,128)}, bf16[64,384]{1,0:T(8,128)(2,1)}, bf16[64,384]...) custom-call(s32[1]{0:T(128)} %bitcast.2.n_ref, ...), custom_call_target="tpu_custom_call" | custom-call | flops 90194313216 | bytes 352321536 | tf_op jit(solution)/shard_map/pallas_call | solution.py:113
  233.8 7.2 %all-to-all-start.1 = ((bf16[16,24,4096]{2,1,0:T(8,128)(2,1)}), bf16[16,24,4096]{2,1,0:T(8,128)(2,1)}, u32[]{:S(2)}, u32[]{:S(2)}) async-start(bf16[16,24,4096]{2,1,0:T(8,128)(2,1)} %bitcast.46), calls=%async_computation.1 | async-start | bytes 6291456 | tf_op jit(solution)/shard_map/all_to_all | solution.py:484
  241.1 70.4 %shard_map.180 = (bf16[384,4096]{1,0:T(8,128)(2,1)}, bf16[384,64]{1,0:T(8,128)(2,1)}, bf16[384,64]{1,0:T(8,128)(2,1)}, f32[32,4096]{1,0:T(8,128)}, f32[32,4096]{...) custom-call(s32[1]{0:T(128)} %bitcast.2.n_ref, ...), custom_call_target="tpu_custom_call" | custom-call | flops 30064771072 | bytes 117440512 | tf_op jit(solution)/shard_map/pallas_call | solution.py:113
  311.5 0.5 collective-permute-start.6
  312.1 0.4 collective-permute-start.7
  312.6 0.4 collective-permute-start.10
  313.0 137.6 %shard_map.181 = bf16[16,24,4096]{2,1,0:T(8,128)(2,1)} custom-call(bf16[384,4096]{1,0:T(8,128)(2,1)} %get-tuple-element.51.ds_ref, bf16[384,384]{1,0:T(8,128)(2,1)} %get-tuple-element.76.spread_ref, bf16[384,64]{1,0:T(8,128)(2,1)} %get-tuple-element.52.qg_ref, bf16[384,64]{1,0:T(8,128)(2,1)} %get-tuple-element.53.qu_ref, bf16[32,4096]{1,0:T(8,128)(2,1)} %bitcast.58, ...), custom_call_target="tpu_custom_call" | custom-call | flops 90194313216 | bytes 234881024 | tf_op jit(solution)/shard_map/pallas_call | solution.py:437
  450.8 3.8 convolution_convert_fusion.3
  454.6 1.7 convolution_convert_fusion.2
  456.3 0.8 add.83
  457.2 0.8 add.85
  458.1 1.9 add.88
  460.0 3.1 add.84
  463.1 3.2 add.86
  466.3 1.5 add.87
  (57 shorter events, 1.0 us)
Async XLA Ops:
  0.6 17.4 %copy-start = (bf16[128,4096]{1,0:T(8,128)(2,1)S(1)}, bf16[128,4096]{1,0:T(8,128)(2,1)}, u32[]{:S(2)}) copy-start(bf16[128,4096]{1,0:T(8,128)(2,1)} %param.14) | copy-start | bytes 3145732
  3.0 15.1 %copy-start.16 = (s32[128]{0:T(128)}, s32[128]{0:T(128)S(1)}, u32[]{:S(2)}) copy-start(s32[128]{0:T(128)S(1)} %fusion.16) | copy-start | bytes 1540
  7.0 9.6 %copy-start.15 = (bf16[2,4096,16]{1,2,0:T(8,128)(2,1)S(1)}, bf16[2,4096,16]{1,2,0:T(8,128)(2,1)}, u32[]{:S(2)}) copy-start(bf16[2,4096,16]{1,2,0:T(8,128)(2,1)} %param.18) | copy-start | bytes 786436
  7.0 10.2 %copy-start.2 = (bf16[2,16,14336]{2,1,0:T(8,128)(2,1)S(1)}, bf16[2,16,14336]{2,1,0:T(8,128)(2,1)}, u32[]{:S(2)}) copy-start(bf16[2,16,14336]{2,1,0:T(8,128)(2,1)} %param.19) | copy-start | bytes 2752516
  7.0 10.6 %copy-start.3 = (bf16[2,16,14336]{2,1,0:T(8,128)(2,1)S(1)}, bf16[2,16,14336]{2,1,0:T(8,128)(2,1)}, u32[]{:S(2)}) copy-start(bf16[2,16,14336]{2,1,0:T(8,128)(2,1)} %param.21) | copy-start | bytes 2752516
  7.0 81.7 %all-to-all-start = ((bf16[16,24,4224]{2,1,0:T(8,128)(2,1)}), bf16[16,24,4224]{2,1,0:T(8,128)(2,1)}, u32[]{:S(2)}, u32[]{:S(2)}) async-start(bf16[16,24,4224]{2,1,0:T(8,128)(2,1)} %bitcast.35), calls=%async_computation | async-start | bytes 6488064 | tf_op jit(solution)/shard_map/all_to_all | solution.py:484
  16.5 74.0 %copy-start.8 = (bf16[2,16,4096]{2,1,0:T(8,128)(2,1)S(1)}, bf16[2,16,4096]{2,1,0:T(8,128)(2,1)}, u32[]{:S(2)}) copy-start(bf16[2,16,4096]{2,1,0:T(8,128)(2,1)} %param.23) | copy-start | bytes 786436
  16.5 74.0 %collective-permute-start = (bf16[32,4096]{1,0:T(8,128)(2,1)S(1)}, bf16[32,4096]{1,0:T(8,128)(2,1)}, u32[]{:S(2)}, u32[]{:S(2)}) collective-permute-start(bf16[32,4096]{1,0:T(8,128)(2,1)S(1)} %bitcast.59), channel_id=1, source_target_pairs={{0,1},{1,0},{2,3},{3,2},{4,5},{5,4},{6,7},{7,6},{8,9},{9,8},{10,11... | collective-permute-start | bytes 786440 | tf_op jit(solution)/shard_map/ppermute | solution.py:499
  17.0 81.1 %collective-permute-start.1 = (bf16[32,4096]{1,0:T(8,128)(2,1)}, bf16[32,4096]{1,0:T(8,128)(2,1)}, u32[]{:S(2)}, u32[]{:S(2)}) collective-permute-start(bf16[32,4096]{1,0:T(8,128)(2,1)} %bitcast.60), channel_id=1, source_target_pairs={{0,1},{1,0},{2,3},{3,2},{4,5},{5,4},{6,7},{7,6},{8,9},{9,8},{10,11... | collective-permute-start | bytes 786440 | tf_op jit(solution)/shard_map/ppermute | solution.py:499
  17.2 81.0 %collective-permute-start.3 = (bf16[32,14336]{1,0:T(8,128)(2,1)S(1)}, bf16[32,14336]{1,0:T(8,128)(2,1)}, u32[]{:S(2)}, u32[]{:S(2)}) collective-permute-start(bf16[32,14336]{1,0:T(8,128)(2,1)S(1)} %bitcast.39), channel_id=1, source_target_pairs={{0,1},{1,0},{2,3},{3,2},{4,5},{5,4},{6,7},{7,6},{8,9},{9,8},{10,11... | collective-permute-start | bytes 2752520 | tf_op jit(solution)/shard_map/ppermute | solution.py:503
  17.5 80.6 %collective-permute-start.4 = (bf16[32,14336]{1,0:T(8,128)(2,1)S(1)}, bf16[32,14336]{1,0:T(8,128)(2,1)}, u32[]{:S(2)}, u32[]{:S(2)}) collective-permute-start(bf16[32,14336]{1,0:T(8,128)(2,1)S(1)} %bitcast.42), channel_id=1, source_target_pairs={{0,1},{1,0},{2,3},{3,2},{4,5},{5,4},{6,7},{7,6},{8,9},{9,8},{10,11... | collective-permute-start | bytes 2752520 | tf_op jit(solution)/shard_map/ppermute | solution.py:503
  17.7 80.5 %collective-permute-start.5 = (bf16[32,14336]{1,0:T(8,128)(2,1)}, bf16[32,14336]{1,0:T(8,128)(2,1)}, u32[]{:S(2)}, u32[]{:S(2)}) collective-permute-start(bf16[32,14336]{1,0:T(8,128)(2,1)} %bitcast.43), channel_id=1, source_target_pairs={{0,1},{1,0},{2,3},{3,2},{4,5},{5,4},{6,7},{7,6},{8,9},{9,8},{10,11... | collective-permute-start | bytes 2752520 | tf_op jit(solution)/shard_map/ppermute | solution.py:499
  90.5 7.6 %collective-permute-start.2 = (bf16[32,4096]{1,0:T(8,128)(2,1)S(1)}, bf16[32,4096]{1,0:T(8,128)(2,1)S(1)}, u32[]{:S(2)}, u32[]{:S(2)}) collective-permute-start(bf16[32,4096]{1,0:T(8,128)(2,1)S(1)} %bitcast.53), channel_id=1, source_target_pairs={{0,1},{1,0},{2,3},{3,2},{4,5},{5,4},{6,7},{7,6},{8,9},{9,8},{10,11... | collective-permute-start | bytes 786440 | tf_op jit(solution)/shard_map/ppermute | solution.py:503
  90.8 143.0 %all-to-all-start.2 = ((bf16[16,24,4096]{2,1,0:T(8,128)(2,1)}), bf16[16,24,4096]{2,1,0:T(8,128)(2,1)}, u32[]{:S(2)}, u32[]{:S(2)}) async-start(bf16[16,24,4096]{2,1,0:T(8,128)(2,1)} %bitcast.36), calls=%async_computation.2 | async-start | bytes 6291456 | tf_op jit(solution)/shard_map/all_to_all | solution.py:484
  233.8 217.0 %all-to-all-start.1 = ((bf16[16,24,4096]{2,1,0:T(8,128)(2,1)}), bf16[16,24,4096]{2,1,0:T(8,128)(2,1)}, u32[]{:S(2)}, u32[]{:S(2)}) async-start(bf16[16,24,4096]{2,1,0:T(8,128)(2,1)} %bitcast.46), calls=%async_computation.1 | async-start | bytes 6291456 | tf_op jit(solution)/shard_map/all_to_all | solution.py:484
  311.5 139.1 %collective-permute-start.6 = (f32[32,4096]{1,0:T(8,128)}, f32[32,4096]{1,0:T(8,128)S(1)}, u32[]{:S(2)}, u32[]{:S(2)}) collective-permute-start(f32[32,4096]{1,0:T(8,128)} %get-tuple-element.59), channel_id=1, source_target_pairs={{0,1},{1,0},{2,3},{3,2},{4,5},{5,4},{6,7},{7,6},{8,9},{9,8},{10,11... | collective-permute-start | bytes 1572872 | tf_op jit(solution)/shard_map/ppermute | solution.py:514
  312.0 145.2 %collective-permute-start.8 = (f32[32,4096]{1,0:T(8,128)}, f32[32,4096]{1,0:T(8,128)S(1)}, u32[]{:S(2)}, u32[]{:S(2)}) collective-permute-start(f32[32,4096]{1,0:T(8,128)} %get-tuple-element.63), channel_id=1, source_target_pairs={{0,1},{1,0},{2,3},{3,2},{4,5},{5,4},{6,7},{7,6},{8,9},{9,8},{10,11... | collective-permute-start | bytes 1572872 | tf_op jit(solution)/shard_map/ppermute | solution.py:514
  312.1 147.8 %collective-permute-start.7 = (f32[32,14336]{1,0:T(8,128)}, f32[32,14336]{1,0:T(8,128)}, u32[]{:S(2)}, u32[]{:S(2)}) collective-permute-start(f32[32,14336]{1,0:T(8,128)} %get-tuple-element.61), channel_id=1, source_target_pairs={{0,1},{1,0},{2,3},{3,2},{4,5},{5,4},{6,7},{7,6},{8,9},{9,8},{10,11... | collective-permute-start | bytes 5505032 | tf_op jit(solution)/shard_map/ppermute | solution.py:514
  312.5 150.6 %collective-permute-start.9 = (f32[32,14336]{1,0:T(8,128)}, f32[32,14336]{1,0:T(8,128)}, u32[]{:S(2)}, u32[]{:S(2)}) collective-permute-start(f32[32,14336]{1,0:T(8,128)} %get-tuple-element.65), channel_id=1, source_target_pairs={{0,1},{1,0},{2,3},{3,2},{4,5},{5,4},{6,7},{7,6},{8,9},{9,8},{10,11... | collective-permute-start | bytes 5505032 | tf_op jit(solution)/shard_map/ppermute | solution.py:514
  312.6 153.6 %collective-permute-start.10 = (f32[32,14336]{1,0:T(8,128)}, f32[32,14336]{1,0:T(8,128)S(1)}, u32[]{:S(2)}, u32[]{:S(2)}) collective-permute-start(f32[32,14336]{1,0:T(8,128)} %get-tuple-element.67), channel_id=1, source_target_pairs={{0,1},{1,0},{2,3},{3,2},{4,5},{5,4},{6,7},{7,6},{8,9},{9,8},{10,11... | collective-permute-start | bytes 5505032 | tf_op jit(solution)/shard_map/ppermute | solution.py:514
  313.0 137.8 %copy-start.17 = (s32[128]{0:T(128)S(1)}, s32[128]{0:T(128)}, u32[]{:S(2)}) copy-start(s32[128]{0:T(128)} %copy-done.16) | copy-start | bytes 1540
  450.6 4.0 copy-start.13
  450.6 7.4 %collective-permute-start.11 = (f32[32,4096]{1,0:T(8,128)}, f32[32,4096]{1,0:T(8,128)}, u32[]{:S(2)}, u32[]{:S(2)}) collective-permute-start(f32[32,4096]{1,0:T(8,128)} %get-tuple-element.69), channel_id=1, source_target_pairs={{0,1},{1,0},{2,3},{3,2},{4,5},{5,4},{6,7},{7,6},{8,9},{9,8},{10,11... | collective-permute-start | bytes 1572872 | tf_op jit(solution)/shard_map/ppermute | solution.py:514
  450.8 3.8 copy-start.4
  454.6 1.8 copy-start.12
  454.6 2.6 copy-start.11
  454.6 1.8 copy-start.14
  454.6 3.5 copy-start.10
  456.3 3.6 copy-start.7
  459.9 3.2 copy-start.6
  463.1 3.2 copy-start.5
  463.1 4.7 copy-start.1
  (1 other events, 0.7 us)
where the time goes:
time: 472 us; the launch traced here: 468 us
  Pallas kernels  343 us (73%)
  waiting for transfers between devices  67.9 us (14%)
  starting transfers between devices  26.6 us (6%)
  other arithmetic  16.5 us (3%)
  matrix products  12.1 us (3%)
    pallas_call x2, Pallas kernels, call(): pl.pallas_call(body, grid_spec=pltpu.PrefetchScalarGridSpec(num_scalar_pr...  205 us
    pallas_call x1, Pallas kernels, dx_all(): pl.pallas_call(functools.partial(dx_kernel, parts), grid=(parts * steps,)...  138 us
    all_to_all x3, waiting for transfers between devices, exchange(): return lax.all_to_all(rows, 'data', 0, 0, tiled=True)  67.9 us
    all_to_all x3, starting transfers between devices, exchange(): return lax.all_to_all(rows, 'data', 0, 0, tiled=True)  23.3 us
    add x6, other arithmetic, layer(): res[j] + lax.ppermute(res[j + 1], 'data', swap)  11.4 us
  transfers between devices with their start and end apart: 15, of which 1 were waited for; matrix products, arithmetic and copies ran while one was open for 4% of the time, Pallas kernels for 73%

commit v1 on v0

--- a/solution.py
+++ b/solution.py
@@ -45,7 +45,7 @@
 
 
 def pieces(width, size):
-    return [slice(j, j + size) for j in range(0, width, size)]
+    return [slice(j, min(j + size, width)) for j in range(0, width, size)]
 
 
 def row_blocks(n, rows, body, when=None):
@@ -220,13 +220,13 @@
 
     @pl.when(i == 0)
     def _():
-        pltpu.make_async_copy(dr_ref, dbuf, sem).start()
+        pltpu.make_async_copy(dr_ref.at[:, pl.ds(0, width)], dbuf, sem).start()
 
     wd, = ring(i, last + 1, [(at_row(wd_hbm, wdb.shape[1]), wdb)], wsem)
 
     @pl.when(i == 0)
     def _():
-        pltpu.make_async_copy(dr_ref, dbuf, sem).wait()
+        pltpu.make_async_copy(dr_ref.at[:, pl.ds(0, width)], dbuf, sem).wait()
 
     def start(r, block):
         take = pack_ref[r, :]
@@ -285,7 +285,7 @@
 
 
 def bwd(scale, n, dr, pack, xs, mask, pgt, put, pdt, bd, wd, g, u, bg, bu, ad, tile=1024, depth=3):
-    rows, width = dr.shape
+    rows, width = dr.shape[0], wd.shape[1]
     hidden = wd.shape[0]
     half = bd[0].shape[0]
     k = 2 * half
@@ -314,7 +314,7 @@
     total = pl.num_programs(0)
     steps = total // parts
     q, t = i // steps, lax.rem(i, steps)
-    _, width = ds_ref.shape
+    rows, width = dgs.shape[0], ds_ref.shape[1]
     tile = wgb.shape[2]
     part = width // parts
     group, cap = back_ref.shape[:2]
@@ -341,7 +341,7 @@
         return pl.ds(pl.multiple_of(s * tile, tile), tile)
 
     def fills(s):
-        pairs = ((dg_lo, dgs, 0), (dg_hi, dgs, LO), (du_lo, dus, 0), (du_hi, dus, LO))
+        pairs = ((dg_lo, dgs, 0), (du_lo, dus, 0), (dg_hi, dgs, LO), (du_hi, dus, LO))[: 4 if rows > LO else 2]
         return [
             pltpu.make_async_copy(src.at[:, cols(s)], dst.at[pl.ds(r, src.shape[0]), cols(s)], psem.at[j, s])
             for j, (src, dst, r) in enumerate(pairs)
@@ -367,10 +367,20 @@
     def _():
         acc[...] = jnp.zeros(acc.shape, F32)
 
-    dg = dgs[:, cols(t)]
-    du = dus[:, cols(t)]
-    for e in pieces(part, CHUNK // 2):
-        acc[:, e] += nt(dg, wg[e, :]) + nt(du, wu[e, :])
+    def add_rows(r):
+        dg = dgs[r, cols(t)]
+        du = dus[r, cols(t)]
+        for e in pieces(part, CHUNK // 2):
+            acc[r, e] += nt(dg, wg[e, :]) + nt(du, wu[e, :])
+
+    def add_block(b, carry):
+        add_rows(pl.ds(pl.multiple_of(b * LANES, LANES), LANES))
+        return carry
+
+    if rows > LO:
+        lax.fori_loop(0, rows // LANES, add_block, 0)
+    else:
+        add_rows(slice(None))
 
     def here(s):
         return pl.ds(pl.multiple_of(s * part, part), part)
@@ -401,7 +411,7 @@
         c = here(q)
         lora = rounded(nn(qg_ref[...], both(ag0, ag1, c)) + nn(qu_ref[...], both(au0, au1, c)))
         dx = (ds_ref[:, c].astype(F32) + acc[...] + lora).astype(BF16)
-        spread = nn(spread_ref[...], dx)
+        spread = nn(spread_ref[:, :rows], dx)
         for p in range(group):
             sendbuf[q, p] = spread[p * cap : (p + 1) * cap].astype(BF16)
 
@@ -423,11 +433,12 @@
                 copy.wait_recv()
 
 
-def dx_all(group, ds, spread, qg, qu, ag, au, wg, wu, dg, du, parts=4, tile=2048, depth=3):
-    rows, width = ds.shape
+def dx_all(rows, group, ds, spread, qg, qu, ag, au, wg, wu, dg, du, parts=8, depth=3):
+    slots, width = ds.shape
     hidden = wg.shape[1]
+    tile = hidden // 4
     half, k = ag[0].shape[0], qg.shape[1]
-    part, cap = width // parts, rows // group
+    part, cap = width // parts, slots // group
     steps = hidden // tile
 
     def fixed(shape):
@@ -437,18 +448,18 @@
     back = pl.pallas_call(
         functools.partial(dx_kernel, parts),
         grid=(parts * steps,),
-        in_specs=[fixed((rows, width)), fixed((rows, rows))] + [fixed((rows, k))] * 2 + [fixed((half, width))] * 4 + [HBM] * 6,
+        in_specs=[fixed((rows, width)), fixed((slots, slots))] + [fixed((rows, k))] * 2 + [fixed((half, width))] * 4 + [HBM] * 6,
         out_specs=HBM,
         out_shape=Shape((group, cap, width), BF16),
         scratch_shapes=[pltpu.VMEM((rows, part), F32)] + [pltpu.VMEM((rows, hidden), BF16)] * 2 + [pltpu.VMEM((parts, group, cap, part), BF16)]
         + [pltpu.VMEM((depth, part, tile), BF16)] * 2
         + [dma((2, depth)), dma((4, steps)), dma((parts, group)), dma((parts, group)), dma((parts,))],
         compiler_params=pltpu.CompilerParams(
-            dimension_semantics=('arbitrary',), vmem_limit_bytes=63_000_000, collective_id=0, has_side_effects=True
+            dimension_semantics=('arbitrary',), vmem_limit_bytes=63_000_000, collective_id=rows // LANES, has_side_effects=True
         ),
         cost_estimate=pl.CostEstimate(flops=4 * rows * width * hidden, bytes_accessed=4 * width * hidden, transcendentals=0),
     )(ds, spread, qg, qu, *ag, *au, wg, wu, *dg, *du)
-    return back.reshape(rows, width)
+    return back.reshape(slots, width)
 
 
 def solution(mesh):
@@ -484,13 +495,15 @@
             return lax.all_to_all(rows, 'data', 0, 0, tiled=True)
 
         xr = exchange(nn(send, jnp.concatenate([x, flags], axis=1)).astype(BF16))
-        packed_dy, xr = lax.optimization_barrier((nn(send, dy).astype(BF16), xr))
-        dr = exchange(packed_dy)
+        packed_dy, xr = lax.optimization_barrier((nn(send, jnp.concatenate([dy, flags], axis=1)).astype(BF16), xr))
 
         valid = jnp.sum(xr[:, width:].astype(F32), axis=1) > 0
         upto = (iota((slots, slots), 0) >= iota((slots, slots), 1)) & valid[None, :]
         place = jnp.where(valid, jnp.sum(jnp.where(upto, 1, 0), axis=1) - 1, -1)
         count = jnp.sum(jnp.where(valid, 1, 0)).astype(jnp.int32).reshape(1)
+        full_load = jnp.broadcast_to((count > LO).astype(BF16), (slots, LANES))
+        dr = exchange(lax.dynamic_update_slice(packed_dy, full_load, (0, width)))
+        any_full = jnp.max(dr[:, width:].astype(F32)) > 0
         pack = (place[None, :] == iota((slots, slots), 0)).astype(BF16)
         spread = (place[:, None] == iota((slots, slots), 1)).astype(BF16)
 
@@ -510,7 +523,8 @@
         ds, qg, qu = res[:3]
         dg, du = res[9:11], res[11:13]
         back = [exchange(out_rows)]
-        back.append(dx_all(group, ds, spread, qg, qu, ag, au, w_gate, w_up, dg, du))
+        args = (ds, spread, qg, qu, ag, au, w_gate, w_up, dg, du)
+        back.append(lax.cond(any_full, functools.partial(dx_all, slots, group), functools.partial(dx_all, LO, group), *args))
         sums = [res[j] + lax.ppermute(res[j + 1], 'data', swap) for j in (3, 5, 7, 13, 15, 17)]
         gag, gau, gbd, gbg, gbu, gad = sums
 

time: 472 us -> 453 us (0.960)
  the two profiles are of different devices: /device:TPU:53 before, /device:TPU:21 now
where the time goes in v1:
time: 453 us; the launch traced here: 449 us
  Pallas kernels  310 us (68%)
  waiting for transfers between devices  76.5 us (17%)
  starting transfers between devices  28 us (6%)
  other arithmetic  19.2 us (4%)
  matrix products  11.3 us (2%)
    pallas_call x2, Pallas kernels, call(): pl.pallas_call(body, grid_spec=pltpu.PrefetchScalarGridSpec(num_scalar_pr...  205 us
    pallas_call x1, Pallas kernels, dx_all(): pl.pallas_call(functools.partial(dx_kernel, parts), grid=(parts * steps,)...  105 us
    all_to_all x3, waiting for transfers between devices, exchange(): return lax.all_to_all(rows, 'data', 0, 0, tiled=True)  67.7 us
    all_to_all x3, starting transfers between devices, exchange(): return lax.all_to_all(rows, 'data', 0, 0, tiled=True)  24.1 us
    add x6, other arithmetic, layer(): res[j] + lax.ppermute(res[j + 1], 'data', swap)  14 us
  transfers between devices with their start and end apart: 15, of which 2 were waited for; matrix products, arithmetic and copies ran while one was open for 5% of the time, Pallas kernels for 69%

profile of v1, /device:TPU:21, one launch (start us, length us, event | category | flops | bytes accessed | tf_op | source)
XLA Modules:
  0.0 449.1 jit_solution(18211412352847691520)
XLA Ops:
  0.6 0.7 and_select_fusion.4
  1.5 0.7 broadcast_add_fusion
  2.3 3.9 convolution_convert_fusion
  6.2 10.9 %all-to-all-start = ((bf16[16,24,4224]{2,1,0:T(8,128)(2,1)}), bf16[16,24,4224]{2,1,0:T(8,128)(2,1)S(1)}, u32[]{:S(2)}, u32[]{:S(2)}) async-start(bf16[16,24,4224]{2,1,0:T(8,128)(2,1)} %bitcast.2), calls=%async_computation | async-start | bytes 6488064 | tf_op jit(solution)/shard_map/all_to_all | solution.py:495
  17.1 0.4 collective-permute-start
  17.7 0.3 collective-permute-start.3
  18.2 0.3 collective-permute-start.5
  18.5 3.9 convolution_convert_fusion.1
  22.4 67.7 %all-to-all-done = bf16[16,24,4224]{2,1,0:T(8,128)(2,1)S(1)} async-done(((bf16[16,24,4224]{2,1,0:T(8,128)(2,1)}), bf16[16,24,4224]{2,1,0:T(8,128)(2,1)S(1)}, u32[]{:S(2)}, u32[]{:S(2)}) %all-to-all-start) | async-done | bytes 3244064 | tf_op jit(solution)/shard_map/all_to_all | solution.py:495
  90.2 0.9 select_reduce_fusion.2
  91.9 1.1 collective-permute-start.2
  93.0 0.7 broadcast_dynamic-update-slice_fusion
  93.6 5.2 %all-to-all-start.2 = ((bf16[16,24,4224]{2,1,0:T(8,128)(2,1)}), bf16[16,24,4224]{2,1,0:T(8,128)(2,1)}, u32[]{:S(2)}, u32[]{:S(2)}) async-start(bf16[16,24,4224]{2,1,0:T(8,128)(2,1)} %bitcast.20), calls=%async_computation.2 | async-start | bytes 6488064 | tf_op jit(solution)/shard_map/all_to_all | solution.py:495
  98.9 0.9 fusion.4
  99.8 134.7 %shard_map.179 = (bf16[384,4096]{1,0:T(8,128)(2,1)}, bf16[384,4096]{1,0:T(8,128)(2,1)}, f32[384,64]{1,0:T(8,128)}, bf16[64,384]{1,0:T(8,128)(2,1)}, bf16[64,384]...) custom-call(s32[1]{0:T(128)} %bitcast.4.n_ref, ...), custom_call_target="tpu_custom_call" | custom-call | flops 90194313216 | bytes 352321536 | tf_op jit(solution)/shard_map/pallas_call | solution.py:113
  234.5 8.1 %all-to-all-start.1 = ((bf16[16,24,4096]{2,1,0:T(8,128)(2,1)}), bf16[16,24,4096]{2,1,0:T(8,128)(2,1)S(1)}, u32[]{:S(2)}, u32[]{:S(2)}) async-start(bf16[16,24,4096]{2,1,0:T(8,128)(2,1)} %bitcast.50), calls=%async_computation.1 | async-start | bytes 6291456 | tf_op jit(solution)/shard_map/all_to_all | solution.py:495
  242.6 70.4 %shard_map.180 = (bf16[384,4096]{1,0:T(8,128)(2,1)}, bf16[384,64]{1,0:T(8,128)(2,1)S(1)}, bf16[384,64]{1,0:T(8,128)(2,1)}, f32[32,4096]{1,0:T(8,128)}, f32[32,40...) custom-call(s32[1]{0:T(128)} %bitcast.4.n_ref, ...), custom_call_target="tpu_custom_call" | custom-call | flops 30064771072 | bytes 117440512 | tf_op jit(solution)/shard_map/pallas_call | solution.py:113
  313.2 0.5 collective-permute-start.9
  313.8 0.4 collective-permute-start.6
  314.3 8.8 %collective-permute-done.6 = f32[32,4096]{1,0:T(8,128)S(1)} collective-permute-done((f32[32,4096]{1,0:T(8,128)}, f32[32,4096]{1,0:T(8,128)S(1)}, u32[]{:S(2)}, u32[]{:S(2)}) %collective-permute-start.6) | collective-permute-done | bytes 524320 | tf_op jit(solution)/shard_map/ppermute | solution.py:528
  323.1 0.8 copy-done.8
  324.1 1.7 convolution_convert_fusion.3
  325.8 1.5 slice_reduce_fusion
  328.0 105.1 %conditional.1 = (bf16[384,4096]{1,0:T(8,128)(2,1)S(1)}) conditional(s32[]{:T(128)} %convert_element_type.43, (bf16[384,4096]{1,0:T(8,128)(2,1)}, bf16[384,384]{1,0:T(8,128)(2,1)S(1)}, bf16[384,64]{1,0:T(8,128)(2,1)S(1)}, bf16[384,64]{1,0:T(8,128)(2,1)}, bf16[32,4096]{1,0:T(8,128)(2,1)}, /*index=5*/bf16[32,4096]{1,0:T(8,128)(2,1)}, ...), branch_computations={%region_5.6_spmd, %region_6.7_spmd} | conditional | flops 90194313216 | bytes 234881024 | solution.py:527
  328.2 104.9 %branch_0_fun.1 = bf16[16,24,4096]{2,1,0:T(8,128)(2,1)S(1)} custom-call(bf16[384,4096]{1,0:T(8,128)(2,1)} %get-tuple-element.41.ds_ref, bf16[384,384]{1,0:T(8,128)(2,1)S(1)} %get-tuple-element.60.spread_ref, bf16[384,64]{1,0:T(8,128)(2,1)S(1)} %get-tuple-element.61.qg_ref, bf16[384,64]{1,0:T(8,128)(2,1)} %get-tuple-element.62.qu_ref, ...), custom_call_target="tpu_custom_call" | custom-call | flops 60129542144 | bytes 234881024 | tf_op jit(solution)/shard_map/cond/branch_0_fun/pallas_call | solution.py:448
  433.2 1.7 convolution_convert_fusion.2
  434.9 0.8 add.83
  435.8 1.9 add.85
  437.7 1.9 add.88
  439.6 3.1 add.84
  442.8 3.1 add.86
  445.9 3.0 add.87
  (50 shorter events, 1.6 us)
Async XLA Ops:
  1.5 17.0 %copy-start.10 = (s32[128]{0:T(128)}, s32[128]{0:T(128)S(1)}, u32[]{:S(2)}) copy-start(s32[128]{0:T(128)S(1)} %get-tuple-element.159) | copy-start | bytes 1540
  6.2 10.9 %copy-start.4 = (bf16[2,4096,16]{1,2,0:T(8,128)(2,1)S(1)}, bf16[2,4096,16]{1,2,0:T(8,128)(2,1)}, u32[]{:S(2)}) copy-start(bf16[2,4096,16]{1,2,0:T(8,128)(2,1)} %param.20) | copy-start | bytes 786436
  6.2 83.9 %all-to-all-start = ((bf16[16,24,4224]{2,1,0:T(8,128)(2,1)}), bf16[16,24,4224]{2,1,0:T(8,128)(2,1)S(1)}, u32[]{:S(2)}, u32[]{:S(2)}) async-start(bf16[16,24,4224]{2,1,0:T(8,128)(2,1)} %bitcast.2), calls=%async_computation | async-start | bytes 6488064 | tf_op jit(solution)/shard_map/all_to_all | solution.py:495
  17.1 74.8 %collective-permute-start = (bf16[32,4096]{1,0:T(8,128)(2,1)S(1)}, bf16[32,4096]{1,0:T(8,128)(2,1)}, u32[]{:S(2)}, u32[]{:S(2)}) collective-permute-start(bf16[32,4096]{1,0:T(8,128)(2,1)S(1)} %bitcast.57), channel_id=1, source_target_pairs={{0,1},{1,0},{2,3},{3,2},{4,5},{5,4},{6,7},{7,6},{8,9},{9,8},{10,11... | collective-permute-start | bytes 786440 | tf_op jit(solution)/shard_map/ppermute | solution.py:512
  17.5 82.3 %collective-permute-start.1 = (bf16[32,4096]{1,0:T(8,128)(2,1)}, bf16[32,4096]{1,0:T(8,128)(2,1)}, u32[]{:S(2)}, u32[]{:S(2)}) collective-permute-start(bf16[32,4096]{1,0:T(8,128)(2,1)} %bitcast.58), channel_id=1, source_target_pairs={{0,1},{1,0},{2,3},{3,2},{4,5},{5,4},{6,7},{7,6},{8,9},{9,8},{10,11... | collective-permute-start | bytes 786440 | tf_op jit(solution)/shard_map/ppermute | solution.py:512
  17.7 82.1 %collective-permute-start.3 = (bf16[32,14336]{1,0:T(8,128)(2,1)}, bf16[32,14336]{1,0:T(8,128)(2,1)}, u32[]{:S(2)}, u32[]{:S(2)}) collective-permute-start(bf16[32,14336]{1,0:T(8,128)(2,1)} %bitcast.41), channel_id=1, source_target_pairs={{0,1},{1,0},{2,3},{3,2},{4,5},{5,4},{6,7},{7,6},{8,9},{9,8},{10,11... | collective-permute-start | bytes 2752520 | tf_op jit(solution)/shard_map/ppermute | solution.py:516
  18.0 81.8 %collective-permute-start.4 = (bf16[32,14336]{1,0:T(8,128)(2,1)}, bf16[32,14336]{1,0:T(8,128)(2,1)}, u32[]{:S(2)}, u32[]{:S(2)}) collective-permute-start(bf16[32,14336]{1,0:T(8,128)(2,1)} %bitcast.44), channel_id=1, source_target_pairs={{0,1},{1,0},{2,3},{3,2},{4,5},{5,4},{6,7},{7,6},{8,9},{9,8},{10,11... | collective-permute-start | bytes 2752520 | tf_op jit(solution)/shard_map/ppermute | solution.py:516
  18.2 81.6 %collective-permute-start.5 = (bf16[32,14336]{1,0:T(8,128)(2,1)}, bf16[32,14336]{1,0:T(8,128)(2,1)}, u32[]{:S(2)}, u32[]{:S(2)}) collective-permute-start(bf16[32,14336]{1,0:T(8,128)(2,1)} %bitcast.47), channel_id=1, source_target_pairs={{0,1},{1,0},{2,3},{3,2},{4,5},{5,4},{6,7},{7,6},{8,9},{9,8},{10,11... | collective-permute-start | bytes 2752520 | tf_op jit(solution)/shard_map/ppermute | solution.py:512
  90.1 3.5 copy-start
  91.9 7.9 %collective-permute-start.2 = (bf16[32,4096]{1,0:T(8,128)(2,1)}, bf16[32,4096]{1,0:T(8,128)(2,1)}, u32[]{:S(2)}, u32[]{:S(2)}) collective-permute-start(bf16[32,4096]{1,0:T(8,128)(2,1)} %bitcast.11.bd0), channel_id=1, source_target_pairs={{0,1},{1,0},{2,3},{3,2},{4,5},{5,4},{6,7},{7,6},{8,9},{9,8},{10,11... | collective-permute-start | bytes 786440 | tf_op jit(solution)/shard_map/ppermute | solution.py:516
  93.6 140.9 %all-to-all-start.2 = ((bf16[16,24,4224]{2,1,0:T(8,128)(2,1)}), bf16[16,24,4224]{2,1,0:T(8,128)(2,1)}, u32[]{:S(2)}, u32[]{:S(2)}) async-start(bf16[16,24,4224]{2,1,0:T(8,128)(2,1)} %bitcast.20), calls=%async_computation.2 | async-start | bytes 6488064 | tf_op jit(solution)/shard_map/all_to_all | solution.py:495
  234.5 89.5 %all-to-all-start.1 = ((bf16[16,24,4096]{2,1,0:T(8,128)(2,1)}), bf16[16,24,4096]{2,1,0:T(8,128)(2,1)S(1)}, u32[]{:S(2)}, u32[]{:S(2)}) async-start(bf16[16,24,4096]{2,1,0:T(8,128)(2,1)} %bitcast.50), calls=%async_computation.1 | async-start | bytes 6291456 | tf_op jit(solution)/shard_map/all_to_all | solution.py:495
  242.6 81.5 %copy-start.11 = (s32[128]{0:T(128)S(1)}, s32[128]{0:T(128)}, u32[]{:S(2)}) copy-start(s32[128]{0:T(128)} %copy-done.10) | copy-start | bytes 1540
  313.0 126.6 %collective-permute-start.7 = (f32[32,14336]{1,0:T(8,128)}, f32[32,14336]{1,0:T(8,128)}, u32[]{:S(2)}, u32[]{:S(2)}) collective-permute-start(f32[32,14336]{1,0:T(8,128)} %get-tuple-element.148), channel_id=1, source_target_pairs={{0,1},{1,0},{2,3},{3,2},{4,5},{5,4},{6,7},{7,6},{8,9},{9,8},{10,11... | collective-permute-start | bytes 5505032 | tf_op jit(solution)/shard_map/ppermute | solution.py:528
  313.2 129.6 %collective-permute-start.9 = (f32[32,14336]{1,0:T(8,128)}, f32[32,14336]{1,0:T(8,128)}, u32[]{:S(2)}, u32[]{:S(2)}) collective-permute-start(f32[32,14336]{1,0:T(8,128)} %get-tuple-element.152), channel_id=1, source_target_pairs={{0,1},{1,0},{2,3},{3,2},{4,5},{5,4},{6,7},{7,6},{8,9},{9,8},{10,11... | collective-permute-start | bytes 5505032 | tf_op jit(solution)/shard_map/ppermute | solution.py:528
  313.6 132.3 %collective-permute-start.10 = (f32[32,14336]{1,0:T(8,128)}, f32[32,14336]{1,0:T(8,128)}, u32[]{:S(2)}, u32[]{:S(2)}) collective-permute-start(f32[32,14336]{1,0:T(8,128)} %get-tuple-element.154), channel_id=1, source_target_pairs={{0,1},{1,0},{2,3},{3,2},{4,5},{5,4},{6,7},{7,6},{8,9},{9,8},{10,11... | collective-permute-start | bytes 5505032 | tf_op jit(solution)/shard_map/ppermute | solution.py:528
  313.8 9.3 %collective-permute-start.6 = (f32[32,4096]{1,0:T(8,128)}, f32[32,4096]{1,0:T(8,128)S(1)}, u32[]{:S(2)}, u32[]{:S(2)}) collective-permute-start(f32[32,4096]{1,0:T(8,128)} %get-tuple-element.146), channel_id=1, source_target_pairs={{0,1},{1,0},{2,3},{3,2},{4,5},{5,4},{6,7},{7,6},{8,9},{9,8},{10,11... | collective-permute-start | bytes 1572872 | tf_op jit(solution)/shard_map/ppermute | solution.py:528
  314.2 121.6 %collective-permute-start.8 = (f32[32,4096]{1,0:T(8,128)}, f32[32,4096]{1,0:T(8,128)}, u32[]{:S(2)}, u32[]{:S(2)}) collective-permute-start(f32[32,4096]{1,0:T(8,128)} %get-tuple-element.150), channel_id=1, source_target_pairs={{0,1},{1,0},{2,3},{3,2},{4,5},{5,4},{6,7},{7,6},{8,9},{9,8},{10,11... | collective-permute-start | bytes 1572872 | tf_op jit(solution)/shard_map/ppermute | solution.py:528
  323.1 0.8 copy-start.8
  323.9 113.8 %collective-permute-start.11 = (f32[32,4096]{1,0:T(8,128)}, f32[32,4096]{1,0:T(8,128)}, u32[]{:S(2)}, u32[]{:S(2)}) collective-permute-start(f32[32,4096]{1,0:T(8,128)} %get-tuple-element.156), channel_id=1, source_target_pairs={{0,1},{1,0},{2,3},{3,2},{4,5},{5,4},{6,7},{7,6},{8,9},{9,8},{10,11... | collective-permute-start | bytes 1572872 | tf_op jit(solution)/shard_map/ppermute | solution.py:528
  328.0 105.1 %copy-start.12 = (s32[128]{0:T(128)S(1)}, s32[128]{0:T(128)}, u32[]{:S(2)}) copy-start(s32[128]{0:T(128)} %copy-done.10) | copy-start | bytes 1540
  433.1 1.8 copy-start.7
  433.1 1.8 copy-start.9
  433.1 2.6 copy-start.6
  433.2 4.5 %copy-start.5 = (f32[32,4096]{1,0:T(8,128)S(1)}, f32[32,4096]{1,0:T(8,128)}, u32[]{:S(2)}) copy-start(f32[32,4096]{1,0:T(8,128)} %get-tuple-element.155) | copy-start | bytes 1572868
  434.9 4.7 %copy-start.3 = (f32[32,14336]{1,0:T(8,128)S(1)}, f32[32,14336]{1,0:T(8,128)}, u32[]{:S(2)}) copy-start(f32[32,14336]{1,0:T(8,128)} %get-tuple-element.147) | copy-start | bytes 5505028
  439.6 3.2 copy-start.2
  442.8 3.2 copy-start.1
